TPU v7x, 256 devices: a whole 4x4x8 slice. The times are simulated.
256 devices in a mesh: row: 32 (over x_hi, z, core), col: 8 (over x_lo, y).
Axes of the slice: x: 4 (x_hi: 2, x_lo: 2; x = x_hi * 2 + x_lo), y: 4, z: 8, core: 2. Of those that a mesh axis runs over, the one named last changes fastest.
Arguments:
- occupied_waves: bfloat16 [1024, 32768], P('row', 'col'), may hold values from -6 to 6
- virtual_waves: bfloat16 [512, 32768], P('row', 'col'), may hold values from -6 to 6
- occupied_decay: float32 [1024], replicated, may hold values from 0.02 to 1
- virtual_decay: float32 [512], replicated, may hold values from 0.02 to 1
Outputs:
- spectrum_real: float32 [1024, 32, 1024], P('row', 'col')
- spectrum_imaginary: float32 [1024, 32, 1024], P('row', 'col')
All inputs are finite; a program needn't handle non-finite values.
Results may differ from a plain program's by a relative error of at most 0.0041.
Values may be sent and summed in bfloat16 or wider, within the bound.
No kernel may reach another device: no remote copies, remote signals or barrier semaphores. Data moves between devices by JAX's collectives and lax.ppermute only.
A program may use at most 64 MiB of HBM per device.

v0:
```python
import math

import jax
import jax.numpy as jnp
from jax import lax
from jax.sharding import PartitionSpec as P

NOCC = 1024
NVIR = 512
NA = 32
NB = 32
NC = 32
ROWS_DEV = 32
NGRID = 32768


def sent_to_all(x, axis):
    devices = lax.axis_size(axis)
    return lax.all_to_all(jnp.broadcast_to(x[None], (devices, *x.shape)), axis, 0, 0, tiled=True)


def over_copies(x, axis):
    return sent_to_all(x, axis).astype(jnp.float32).sum(axis=0)


def in_blocks(x, dim, devices):
    shape = x.shape
    parts = x.reshape(*shape[:dim], devices, shape[dim] // devices, *shape[dim + 1 :])
    return jnp.moveaxis(parts, dim, 0)


def laid_out(parts, dim):
    shape = list(parts.shape[1:])
    shape[dim] *= parts.shape[0]
    return jnp.moveaxis(parts, 0, dim).reshape(shape)


def exchange_both(x, axis, axes, splits, concats):
    sizes = [lax.axis_size(a) for a in axes]
    parts = in_blocks(x, splits[0], sizes[0])
    parts = jnp.moveaxis(in_blocks(parts, splits[1] + 1, sizes[1]), 0, 1)
    inside = parts.shape[2:]
    parts = parts.reshape(-1, *inside)
    parts = lax.all_to_all(parts, axis, split_axis=0, concat_axis=0, tiled=True)
    parts = laid_out(parts.reshape(*sizes, *inside), concats[0] + 1)
    return laid_out(parts, concats[1])


def tables(length):
    index = jnp.arange(length, dtype=jnp.int32)
    phase = index[:, None] * index[None, :] % length
    angle = phase.astype(jnp.float32) * (2.0 * math.pi / length)
    return (jnp.cos(angle), jnp.sin(angle))


def apply_table(form, data, table):
    return jnp.einsum(form, data, table, precision=lax.Precision.HIGHEST)


def real_step(data, form, length):
    cosine, sine = tables(length)
    return (apply_table(form, data, cosine), -apply_table(form, data, sine))


def complex_step(real_part, imag_part, form, length):
    cosine, sine = tables(length)
    new_real = apply_table(form, real_part, cosine) + apply_table(form, imag_part, sine)
    new_imag = apply_table(form, imag_part, cosine) - apply_table(form, real_part, sine)
    return (new_real, new_imag)


def scale_rows(waves, decay):
    return (waves * decay[:, None]).astype(jnp.bfloat16)


def place(waves, window, start_col):
    block_cols = waves.shape[1]
    buffer = jnp.zeros((waves.shape[0], window + block_cols), jnp.bfloat16)
    buffer = lax.dynamic_update_slice(buffer, waves, (jnp.int32(0), start_col))
    return buffer[:, :window]


def on_device(occupied_waves, virtual_waves, occupied_decay, virtual_decay):
    block_cols = occupied_waves.shape[1]
    row_count = lax.axis_size("row")
    contract = (((0,), (0,)), ((), ()))
    factor = -1.0 / math.sqrt(NOCC * NVIR)
    window = ROWS_DEV * row_count
    start_col = lax.axis_index("col") * block_cols
    plane_cols = NB * NC
    per_col = block_cols // plane_cols
    spread = row_count // per_col
    sub_rows = ROWS_DEV // spread

    def spread_planes(waves):
        share = waves.shape[0]
        shaped = waves.reshape(share, per_col, 1, plane_cols)
        shaped = jnp.broadcast_to(shaped, (share, per_col, spread, plane_cols))
        return shaped.reshape(share, row_count * plane_cols)

    def pick_rows(waves):
        share = waves.shape[0]
        shaped = place(waves, window, start_col).reshape(share, row_count, spread, sub_rows)
        shaped = jnp.transpose(shaped, (0, 2, 1, 3))[:, None]
        shaped = jnp.broadcast_to(shaped, (share, per_col, spread, row_count, sub_rows))
        return shaped.reshape(share, row_count * row_count * sub_rows)

    plane_occ, plane_vir = (
        lax.all_to_all(
            spread_planes(occupied_waves), "row", split_axis=1, concat_axis=0, tiled=True
        ),
        lax.all_to_all(
            spread_planes(virtual_waves), "row", split_axis=1, concat_axis=0, tiled=True
        ),
    )
    part_occ, part_vir = (
        lax.all_to_all(pick_rows(occupied_waves), "row", split_axis=1, concat_axis=0, tiled=True),
        lax.all_to_all(pick_rows(virtual_waves), "row", split_axis=1, concat_axis=0, tiled=True),
    )
    occ_rows, vir_rows = (
        over_copies(part_occ.astype(jnp.float32).astype(jnp.bfloat16), "col").astype(jnp.float32),
        over_copies(part_vir.astype(jnp.float32).astype(jnp.bfloat16), "col").astype(jnp.float32),
    )
    occ_rows = scale_rows(occ_rows, occupied_decay)
    vir_rows = scale_rows(vir_rows, virtual_decay)
    green_occ = lax.dot_general(plane_occ, occ_rows, contract, preferred_element_type=jnp.float32)
    green_vir = lax.dot_general(plane_vir, vir_rows, contract, preferred_element_type=jnp.float32)
    polar = green_occ * green_vir * factor
    cube = polar.reshape(1, NB, NC, row_count * sub_rows)
    real_part, imag_part = real_step(cube, "abcr,cw->wabr", NC)
    real_part, imag_part = complex_step(real_part, imag_part, "wabr,bv->wavr", NB)
    blocked = (NC, 1, NB, row_count, sub_rows)
    real_part, imag_part = (
        exchange_both(
            real_part.reshape(blocked).astype(jnp.bfloat16),
            ("row", "col"),
            ("row", "col"),
            (3, 0),
            (3, 1),
        ).astype(jnp.float32),
        exchange_both(
            imag_part.reshape(blocked).astype(jnp.bfloat16),
            ("row", "col"),
            ("row", "col"),
            (3, 0),
            (3, 1),
        ).astype(jnp.float32),
    )

    def settle(part):
        kc_share = part.shape[0]
        part = part.reshape(kc_share, part.shape[1], NB, per_col, spread, sub_rows)
        part = jnp.transpose(part, (0, 1, 3, 2, 4, 5))
        return part.reshape(kc_share, NA, NB, ROWS_DEV)

    real_part, imag_part = complex_step(settle(real_part), settle(imag_part), "wavr,au->rwuv", NA)
    normal = 1.0 / math.sqrt(NGRID)
    final_shape = (real_part.shape[0], real_part.shape[1], NA * NB)
    return ((real_part * normal).reshape(final_shape), (imag_part * normal).reshape(final_shape))


def solution(mesh):
    in_specs = (P("row", "col"), P("row", "col"), P(), P())
    out_specs = (P("row", "col", None), P("row", "col", None))
    return jax.shard_map(
        on_device, mesh=mesh, in_specs=in_specs, out_specs=out_specs, check_vma=False
    )
```

profile of v0, /device:TPU:32, one launch (start us, length us, event | category | flops | bytes accessed | tf_op | source)
XLA Modules:
  0.0 264.2 jit_solution(17374565482399408237)
XLA Ops:
  0.6 1.4 copy.76
  2.0 0.2 broadcast_in_dim.30
  2.2 0.1 constant_dynamic-update-slice_fusion
  2.4 0.1 broadcast_in_dim.31
  2.6 1.7 copy.78
  4.3 11.2 %all-to-all-start.3 = ((bf16[16,32,128]{2,0,1:T(8,128)(2,1)}), bf16[16,32,128]{2,0,1:T(8,128)(2,1)S(1)}, u32[]{:S(2)}, u32[]{:S(2)}) async-start(bf16[16,32,128]{2,0,1:T(8,128)(2,1)} %copy.78), calls=%async_computation.3 | async-start | bytes 262144 | tf_op jit(solution)/shard_map/all_to_all | solution.py:118
  15.5 0.5 copy.72
  16.0 0.2 broadcast_in_dim.24
  16.2 0.1 constant_dynamic-update-slice_fusion.1
  16.4 0.1 broadcast_in_dim.25
  16.5 1.1 copy.74
  17.6 8.7 %all-to-all-done.3 = bf16[16,32,128]{2,0,1:T(8,128)(2,1)S(1)} async-done(((bf16[16,32,128]{2,0,1:T(8,128)(2,1)}), bf16[16,32,128]{2,0,1:T(8,128)(2,1)S(1)}, u32[]{:S(2)}, u32[]{:S(2)}) %all-to-all-start.3) | async-done | bytes 131104 | tf_op jit(solution)/shard_map/all_to_all | solution.py:118
  26.3 17.7 %all_to_all.90 = bf16[32,32,128]{2,0,1:T(8,128)(2,1)S(1)} all-to-all(bf16[32,32,128]{2,0,1:T(8,128)(2,1)S(1)} %copy.74), channel_id=1, replica_groups=mesh['row'=32,'col'=8] {'row'}, dimensions={1} | all-to-all | bytes 524288 | tf_op jit(solution)/shard_map/all_to_all | solution.py:117
  44.0 0.1 broadcast_in_dim.65
  44.2 19.1 %all_to_all.91 = bf16[8,512,128]{2,1,0:T(8,128)(2,1)S(1)} all-to-all(bf16[8,512,128]{2,1,0:T(8,128)(2,1)S(1)} %broadcast_in_dim.65), channel_id=1, replica_groups=mesh['row'=32,'col'=8] {'col'}, dimensions={0} | all-to-all | bytes 2097152 | tf_op jit(solution)/shard_map/all_to_all | solution.py:19
  63.3 1.6 broadcast_in_dim.27
  64.9 3.6 %all-to-all-start.1 = ((bf16[8,1024,128]{2,1,0:T(8,128)(2,1)}), bf16[8,1024,128]{2,1,0:T(8,128)(2,1)S(1)}, u32[]{:S(2)}, u32[]{:S(2)}) async-start(bf16[8,1024,128]{2,1,0:T(8,128)(2,1)} %broadcast_in_dim.27), calls=%async_computation.1 | async-start | bytes 4194304 | tf_op jit(solution)/shard_map/all_to_all | solution.py:19
  68.5 0.7 copy.123
  69.2 23.2 %all-to-all-done.1 = bf16[8,1024,128]{2,1,0:T(8,128)(2,1)S(1)} async-done(((bf16[8,1024,128]{2,1,0:T(8,128)(2,1)}), bf16[8,1024,128]{2,1,0:T(8,128)(2,1)S(1)}, u32[]{:S(2)}, u32[]{:S(2)}) %all-to-all-start.1) | async-done | bytes 2097184 | tf_op jit(solution)/shard_map/all_to_all | solution.py:19
  92.5 2.5 broadcast_in_dim.29
  95.0 6.1 %all-to-all-start.2 = ((bf16[32,32,1024]{2,0,1:T(8,128)(2,1)}), bf16[32,32,1024]{2,0,1:T(8,128)(2,1)}, u32[]{:S(2)}, u32[]{:S(2)}) async-start(bf16[32,32,1024]{2,0,1:T(8,128)(2,1)} %bitcast.125), calls=%async_computation.2 | async-start | bytes 4194304 | tf_op jit(solution)/shard_map/all_to_all | solution.py:109
  101.2 53.0 %all-to-all-done.2 = bf16[32,32,1024]{2,0,1:T(8,128)(2,1)} async-done(((bf16[32,32,1024]{2,0,1:T(8,128)(2,1)}), bf16[32,32,1024]{2,0,1:T(8,128)(2,1)}, u32[]{:S(2)}, u32[]{:S(2)}) %all-to-all-start.2) | async-done | bytes 2097184 | tf_op jit(solution)/shard_map/all_to_all | solution.py:109
  154.1 1.1 broadcast_in_dim.67
  155.2 4.6 %all-to-all-start.5 = ((bf16[16,32,1024]{2,0,1:T(8,128)(2,1)}), bf16[16,32,1024]{2,0,1:T(8,128)(2,1)}, u32[]{:S(2)}, u32[]{:S(2)}) async-start(bf16[16,32,1024]{2,0,1:T(8,128)(2,1)} %bitcast.136), calls=%async_computation.5 | async-start | bytes 2097152 | tf_op jit(solution)/shard_map/all_to_all | solution.py:112
  159.9 0.1 convert_reduce_fusion.1
  160.0 0.3 convert_reduce_fusion
  160.4 0.2 copy-done.2
  160.6 2.3 fusion.12
  162.9 26.4 %all-to-all-done.5 = bf16[16,32,1024]{2,0,1:T(8,128)(2,1)} async-done(((bf16[16,32,1024]{2,0,1:T(8,128)(2,1)}), bf16[16,32,1024]{2,0,1:T(8,128)(2,1)}, u32[]{:S(2)}, u32[]{:S(2)}) %all-to-all-start.5) | async-done | bytes 1048608 | tf_op jit(solution)/shard_map/all_to_all | solution.py:112
  189.3 1.7 fusion.1
  191.0 0.2 copy.80
  191.2 0.7 convolution_negate_fusion
  191.9 0.7 fusion.29
  192.5 0.9 fusion.6
  193.4 0.9 fusion.4
  194.3 1.4 copy.91
  195.8 0.1 copy.92
  195.9 0.4 copy.125
  196.2 1.4 reshape.155
  197.6 5.5 %all-to-all-start.7 = ((bf16[256,2,256]{2,1,0:T(2,128)(2,1)}), bf16[256,2,256]{2,1,0:T(2,128)(2,1)S(1)}, u32[]{:S(2)}, u32[]{:S(2)}) async-start(bf16[256,2,256]{2,1,0:T(2,128)(2,1)} %reshape.155), calls=%async_computation.7 | async-start | bytes 524288 | tf_op jit(solution)/shard_map/all_to_all | solution.py:44
  203.1 0.9 fusion.10
  204.0 0.9 fusion.5
  205.0 1.4 copy.83
  206.5 0.4 copy.126
  206.9 1.4 reshape.153
  208.2 9.5 %all-to-all-done.7 = bf16[256,2,256]{2,1,0:T(2,128)(2,1)S(1)} async-done(((bf16[256,2,256]{2,1,0:T(2,128)(2,1)}), bf16[256,2,256]{2,1,0:T(2,128)(2,1)S(1)}, u32[]{:S(2)}, u32[]{:S(2)}) %all-to-all-start.7) | async-done | bytes 262176 | tf_op jit(solution)/shard_map/all_to_all | solution.py:44
  217.8 6.4 %all-to-all-start.6 = ((bf16[256,2,256]{2,1,0:T(2,128)(2,1)}), bf16[256,2,256]{2,1,0:T(2,128)(2,1)S(1)}, u32[]{:S(2)}, u32[]{:S(2)}) async-start(bf16[256,2,256]{2,1,0:T(2,128)(2,1)} %reshape.153), calls=%async_computation.6 | async-start | bytes 524288 | tf_op jit(solution)/shard_map/all_to_all | solution.py:44
  224.2 0.5 reshape.156
  224.7 0.3 copy.94
  225.0 0.8 copy.95
  225.8 1.7 copy.96
  227.5 11.3 %all-to-all-done.6 = bf16[256,2,256]{2,1,0:T(2,128)(2,1)S(1)} async-done(((bf16[256,2,256]{2,1,0:T(2,128)(2,1)}), bf16[256,2,256]{2,1,0:T(2,128)(2,1)S(1)}, u32[]{:S(2)}, u32[]{:S(2)}) %all-to-all-start.6) | async-done | bytes 262176 | tf_op jit(solution)/shard_map/all_to_all | solution.py:44
  238.8 0.5 reshape.154
  239.3 0.3 copy.86
  239.6 0.8 copy.87
  240.4 1.7 copy.88
  242.1 1.0 fusion.22
  243.2 2.4 fusion.20
  245.5 2.4 multiply_bitcast_fusion.1
  248.0 4.1 %copy.105 = f32[32,4,32,32]{3,2,1,0:T(8,128)} copy(f32[32,4,32,32]{0,2,3,1:T(8,128)} %multiply_bitcast_fusion.1) | data formatting | bytes 1048576
  252.0 3.1 %reshape.151 = f32[32,4,1024]{2,1,0:T(4,128)} reshape(f32[32,4,32,32]{3,2,1,0:T(8,128)} %copy.105) | data formatting | bytes 1048576
  255.2 4.0 %multiply_bitcast_fusion = f32[32,4,32,32]{0,2,3,1:T(8,128)} fusion(f32[32,4,32,32]{3,0,2,1:T(8,128)} %fusion.20, bf16[4,32,32,32]{3,1,2,0:T(8,128)(2,1)S(1)} %copy.88), kind=kOutput, calls=%fused_computation.1 | convolution fusion | flops 50608128 | bytes 1310720 | tf_op jit(solution)/shard_map/wavr,au->rwuv/dot_general | solution.py:57
  259.2 3.2 %copy.106 = f32[32,4,32,32]{3,2,1,0:T(8,128)S(1)} copy(f32[32,4,32,32]{0,2,3,1:T(8,128)} %multiply_bitcast_fusion) | data formatting | bytes 1048576
  262.4 1.7 reshape.152
  (13 shorter events, 0.2 us)
Async XLA Ops:
  2.4 13.1 %copy-start = (bf16[32,4096]{1,0:T(8,128)(2,1)S(1)}, bf16[32,4096]{1,0:T(8,128)(2,1)}, u32[]{:S(2)}) copy-start(bf16[32,4096]{1,0:T(8,128)(2,1)} %param.4) | copy-start | bytes 786436
  4.3 22.0 %all-to-all-start.3 = ((bf16[16,32,128]{2,0,1:T(8,128)(2,1)}), bf16[16,32,128]{2,0,1:T(8,128)(2,1)S(1)}, u32[]{:S(2)}, u32[]{:S(2)}) async-start(bf16[16,32,128]{2,0,1:T(8,128)(2,1)} %copy.78), calls=%async_computation.3 | async-start | bytes 262144 | tf_op jit(solution)/shard_map/all_to_all | solution.py:118
  64.9 27.6 %all-to-all-start.1 = ((bf16[8,1024,128]{2,1,0:T(8,128)(2,1)}), bf16[8,1024,128]{2,1,0:T(8,128)(2,1)S(1)}, u32[]{:S(2)}, u32[]{:S(2)}) async-start(bf16[8,1024,128]{2,1,0:T(8,128)(2,1)} %broadcast_in_dim.27), calls=%async_computation.1 | async-start | bytes 4194304 | tf_op jit(solution)/shard_map/all_to_all | solution.py:19
  95.0 6.1 %copy-start.1 = (bf16[16,4096]{1,0:T(8,128)(2,1)S(1)}, bf16[16,4096]{1,0:T(8,128)(2,1)}, u32[]{:S(2)}) copy-start(bf16[16,4096]{1,0:T(8,128)(2,1)} %param.5) | copy-start | bytes 393220
  95.0 59.1 %all-to-all-start.2 = ((bf16[32,32,1024]{2,0,1:T(8,128)(2,1)}), bf16[32,32,1024]{2,0,1:T(8,128)(2,1)}, u32[]{:S(2)}, u32[]{:S(2)}) async-start(bf16[32,32,1024]{2,0,1:T(8,128)(2,1)} %bitcast.125), calls=%async_computation.2 | async-start | bytes 4194304 | tf_op jit(solution)/shard_map/all_to_all | solution.py:109
  155.2 34.0 %all-to-all-start.5 = ((bf16[16,32,1024]{2,0,1:T(8,128)(2,1)}), bf16[16,32,1024]{2,0,1:T(8,128)(2,1)}, u32[]{:S(2)}, u32[]{:S(2)}) async-start(bf16[16,32,1024]{2,0,1:T(8,128)(2,1)} %bitcast.136), calls=%async_computation.5 | async-start | bytes 2097152 | tf_op jit(solution)/shard_map/all_to_all | solution.py:112
  159.9 0.7 copy-start.2
  160.4 28.9 %copy-start.3 = (f32[512]{0:T(512)S(1)}, f32[512]{0:T(512)}, u32[]{:S(2)}) copy-start(f32[512]{0:T(512)} %param.7) | copy-start | bytes 6148
  197.6 20.2 %all-to-all-start.7 = ((bf16[256,2,256]{2,1,0:T(2,128)(2,1)}), bf16[256,2,256]{2,1,0:T(2,128)(2,1)S(1)}, u32[]{:S(2)}, u32[]{:S(2)}) async-start(bf16[256,2,256]{2,1,0:T(2,128)(2,1)} %reshape.155), calls=%async_computation.7 | async-start | bytes 524288 | tf_op jit(solution)/shard_map/all_to_all | solution.py:44
  217.8 21.0 %all-to-all-start.6 = ((bf16[256,2,256]{2,1,0:T(2,128)(2,1)}), bf16[256,2,256]{2,1,0:T(2,128)(2,1)S(1)}, u32[]{:S(2)}, u32[]{:S(2)}) async-start(bf16[256,2,256]{2,1,0:T(2,128)(2,1)} %reshape.153), calls=%async_computation.6 | async-start | bytes 524288 | tf_op jit(solution)/shard_map/all_to_all | solution.py:44
where the time goes:
time: 267 us; the launch traced here: 264 us
  waiting for transfers between devices  132 us (49%)
  local copies, waits for them, and re-layouts  37.5 us (14%)
  starting transfers between devices  37.5 us (14%)
  blocking collectives  36.8 us (14%)
  matrix products  18.8 us (7%)
    all_to_all x1, waiting for transfers between devices, on_device(): lax.all_to_all(spread_planes(occupied_waves), 'row', split_axis=1, concat...  53 us
    all_to_all x1, waiting for transfers between devices, on_device(): lax.all_to_all(spread_planes(virtual_waves), 'row', split_axis=1, concat_...  26.4 us
    all_to_all x1, waiting for transfers between devices, sent_to_all(): lax.all_to_all(jnp.broadcast_to(x[None], (devices, *x.shape)), axis, 0, 0...  23.2 us
    all_to_all x2, waiting for transfers between devices, exchange_both(): parts = lax.all_to_all(parts, axis, split_axis=0, concat_axis=0, tiled=True)  20.9 us
    all_to_all x1, blocking collectives, sent_to_all(): lax.all_to_all(jnp.broadcast_to(x[None], (devices, *x.shape)), axis, 0, 0...  19.1 us
    unnamed x18, local copies, waits for them, and re-layouts  18 us
    all_to_all x1, blocking collectives, on_device(): lax.all_to_all(pick_rows(occupied_waves), 'row', split_axis=1, concat_axi...  17.7 us
    dot_general x10, matrix products, apply_table(): return jnp.einsum(form, data, table, precision=lax.Precision.HIGHEST)  14.8 us
  transfers between devices with their start and end apart: 6, of which 6 were waited for; matrix products, arithmetic and copies ran while one was open for 5% of the time, Pallas kernels for 0%

commit v1 on v0

v1 whole, which is shorter than its diff:
```python
import math

import jax
import jax.numpy as jnp
import numpy as np
from jax import lax
from jax.experimental import pallas as pl
from jax.experimental.pallas import tpu as pltpu
from jax.sharding import Mesh, PartitionSpec as P

NOCC = 1024
NVIR = 512
NGRID = 32768
POLAR_FACTOR = -1.0 / math.sqrt(NOCC * NVIR)
NORMAL = 1.0 / math.sqrt(NGRID)
FINE = ("xh", "z", "c", "xl", "y")
FINE_SIZES = (2, 8, 2, 2, 4)
ROW = ("xh", "z", "c")
COL = ("xl", "y")
SAME_CORE = ("xh", "z", "xl", "y")
BF16 = jnp.bfloat16
F32 = jnp.float32


def split_table(table):
    high = table.astype(np.float32).astype(jnp.bfloat16)
    low = (table - high.astype(np.float64)).astype(np.float32).astype(jnp.bfloat16)
    return high, low


def rotation(phase):
    cosine, sine = np.cos(phase), np.sin(phase)
    return np.array([[cosine, sine], [-sine, cosine]])


def c_table():
    kc = np.arange(32).reshape(8, 4)
    turn = rotation(2 * np.pi * (kc[..., None] * np.arange(32) % 32) / 32)[:, 0]
    full = np.einsum("pjic,bd->ijpbdc", turn, np.eye(8))
    return split_table(full.reshape(512, 256))


def a_table():
    ka = np.arange(32)
    turn = rotation(2 * np.pi * (ka[:, None] * ka[None, :] % 32) / 32)
    turn = turn.reshape(2, 2, 8, 4, 8, 4)
    full = np.einsum("pqghck,bd->ghpbkcqd", turn, np.eye(8))
    return split_table(full.reshape(512, 512))


def b_table():
    kb = np.arange(32)
    turn = rotation(2 * np.pi * (kb[:, None] * kb[None, :] % 32) / 32) * NORMAL
    turn = turn.reshape(2, 2, 32, 4, 8)
    full = np.einsum("pqkBb,hj->Bhqbpjk", turn, np.eye(4))
    return split_table(full.reshape(256, 256))


def dot(a, b):
    return lax.dot_general(a, b, (((1,), (0,)), ((), ())), preferred_element_type=F32)


def prepare_kernel(place_ref, occ_decay_ref, vir_decay_ref, occ_ref, vir_ref, out_ref):
    row = place_ref[0]

    def column(decay_ref, count):
        index = lax.broadcasted_iota(jnp.int32, (count, 128), 0)
        out = jnp.zeros((count, 128), F32)
        for i in range(count):
            out = jnp.where(index == i, decay_ref[row * count + i], out)
        return out

    def chunks(ref, decay):
        count = ref.shape[0]
        scaled = [
            ref[:, 128 * t : 128 * (t + 1)].astype(F32) * decay for t in range(8)
        ]
        for y in range(4):
            first, second = scaled[2 * y], scaled[2 * y + 1]
            for h in range(2):
                pieces = [
                    part[:, 64 * u + 32 * h : 64 * u + 32 * h + 32]
                    for part in (first, second)
                    for u in range(2)
                ]
                yield y, h, jnp.concatenate(pieces, axis=1)

    for y, h, rows in chunks(occ_ref, column(occ_decay_ref, 32)):
        for xl in range(2):
            out_ref[4 * xl + y, h, 0:16, :] = rows[16 * xl : 16 * xl + 16].astype(BF16)
    for y, h, rows in chunks(vir_ref, column(vir_decay_ref, 16)):
        for xl in range(2):
            out_ref[4 * xl + y, h, 16:24, :] = rows[8 * xl : 8 * xl + 8].astype(BF16)


def prepare(place, occ_decay, vir_decay, occ, vir):
    smem = pl.BlockSpec(memory_space=pltpu.SMEM)
    return pl.pallas_call(
        prepare_kernel,
        grid=(1,),
        out_shape=jax.ShapeDtypeStruct((8, 2, 24, 128), BF16),
        in_specs=[
            smem,
            smem,
            smem,
            pl.BlockSpec((32, 1024), lambda i: (0, 0)),
            pl.BlockSpec((16, 1024), lambda i: (0, 0)),
        ],
        out_specs=pl.BlockSpec((8, 2, 24, 128), lambda i: (0, 0, 0, 0)),
        name="prepare",
    )(place, occ_decay, vir_decay, occ, vir)


def pack_kernel(occ_ref, vir_ref, rows_ref, out_ref):
    for p in range(32):
        out_ref[p, 0:32, :] = occ_ref[:, 128 * p : 128 * (p + 1)]
        out_ref[p, 32:48, :] = vir_ref[:, 128 * p : 128 * (p + 1)]
        out_ref[p, 48:72, :] = rows_ref[0, p % 2]


def pack(occ, vir, rows):
    return pl.pallas_call(
        pack_kernel,
        grid=(1,),
        out_shape=jax.ShapeDtypeStruct((32, 72, 128), BF16),
        in_specs=[
            pl.BlockSpec((32, 4096), lambda i: (0, 0)),
            pl.BlockSpec((16, 4096), lambda i: (0, 0)),
            pl.BlockSpec((1, 2, 24, 128), lambda i: (0, 0, 0, 0)),
        ],
        out_specs=pl.BlockSpec((32, 72, 128), lambda i: (0, 0, 0)),
        name="pack",
    )(occ, vir, rows)


def polar_kernel(core_ref, own_ref, other_ref, rows_ref, high_ref, low_ref, out_ref, polar_ref):
    core = core_ref[0]
    for half, ref in enumerate((own_ref, other_ref)):
        start = pl.multiple_of((core if half == 0 else 1 - core) * 128, 128)
        occ = ref[0:1024, :].T
        vir = ref[1024:1536, :].T
        for y in range(4):
            green_occ = dot(occ[:, :512], rows_ref[y, :512]) + dot(
                occ[:, 512:], rows_ref[4 + y, :512]
            )
            green_vir = dot(vir[:, :256], rows_ref[y, 512:]) + dot(
                vir[:, 256:], rows_ref[4 + y, 512:]
            )
            polar_ref[pl.ds(start, 128), 128 * y : 128 * (y + 1)] = (
                green_occ * green_vir * POLAR_FACTOR
            )
    polar = polar_ref[...]
    polar_high = polar.astype(BF16)
    polar_low = (polar - polar_high.astype(F32)).astype(BF16)
    spectrum = (
        dot(high_ref[...], polar_high)
        + dot(high_ref[...], polar_low)
        + dot(low_ref[...], polar_high)
    )
    for m in range(16):
        pieces = [spectrum[128 * i : 128 * (i + 1), 32 * m : 32 * (m + 1)] for i in range(4)]
        out_ref[m] = jnp.concatenate(pieces, axis=1).astype(BF16)


def polar_messages(core, own, other, rows):
    high, low = c_table()
    vmem = pl.BlockSpec(memory_space=pltpu.VMEM)
    return pl.pallas_call(
        polar_kernel,
        out_shape=jax.ShapeDtypeStruct((16, 128, 128), BF16),
        in_specs=[pl.BlockSpec(memory_space=pltpu.SMEM)] + [vmem] * 5,
        out_specs=vmem,
        scratch_shapes=[pltpu.VMEM((256, 512), F32)],
        name="polar",
    )(core, own, other, rows, high, low)


def finish_kernel(x_ref, a_high_ref, a_low_ref, b_high_ref, b_low_ref, real_ref, imag_ref):
    planes = []
    for block in range(4):
        x = jnp.concatenate(
            [x_ref[128 * (4 * k + block) : 128 * (4 * k + block + 1), :] for k in range(4)], axis=0
        )
        planes.append(dot(a_high_ref[...], x) + dot(a_low_ref[...], x))
    for g in range(8):
        z = jnp.concatenate([plane[64 * g : 64 * (g + 1)] for plane in planes], axis=0).T
        z_high = z.astype(BF16)
        z_low = (z - z_high.astype(F32)).astype(BF16)
        out = (
            dot(z_high, b_high_ref[...])
            + dot(z_high, b_low_ref[...])
            + dot(z_low, b_high_ref[...])
        )
        for i in range(4):
            real_ref[:, i, 128 * g : 128 * (g + 1)] = out[32 * i : 32 * (i + 1), :128]
            imag_ref[:, i, 128 * g : 128 * (g + 1)] = out[32 * i : 32 * (i + 1), 128:]


def finish(x):
    vmem = pl.BlockSpec(memory_space=pltpu.VMEM)
    shape = jax.ShapeDtypeStruct((32, 4, 1024), F32)
    return pl.pallas_call(
        finish_kernel,
        out_shape=(shape, shape),
        in_specs=[vmem] * 5,
        out_specs=(vmem, vmem),
        name="finish",
    )(x, *a_table(), *b_table())


def on_device(occ, vir, occ_decay, vir_decay):
    row = lax.axis_index(ROW).astype(jnp.int32).reshape(1)
    core = lax.axis_index("c").astype(jnp.int32).reshape(1)
    scattered = lax.all_to_all(prepare(row, occ_decay, vir_decay, occ, vir), COL, 0, 0, tiled=True)
    arrived = lax.all_to_all(pack(occ, vir, scattered), ROW, 0, 0, tiled=True)

    def by_half(part, count):
        part = part.reshape(32, 2, count // 2, 128)
        return jnp.transpose(part, (1, 0, 2, 3)).reshape(32 * count, 128)

    own = jnp.concatenate([by_half(arrived[:, :32], 32), by_half(arrived[:, 32:48], 16)], axis=0)
    share = jnp.concatenate(
        [arrived[:, 48:64].reshape(512, 128), arrived[:, 64:72].reshape(256, 128)], axis=0
    )
    other = lax.ppermute(own, "c", [(0, 1), (1, 0)])
    rows = lax.all_to_all(jnp.broadcast_to(share[None], (8, 768, 128)), COL, 0, 0, tiled=True)
    messages = polar_messages(core, own, other, rows).reshape(128, 16, 128)
    received = lax.all_to_all(messages, SAME_CORE, 0, 0, tiled=True)
    return finish(received.reshape(2048, 128))


def solution(mesh):
    fine = Mesh(mesh.devices.reshape(FINE_SIZES), FINE)
    return jax.shard_map(
        on_device,
        mesh=fine,
        in_specs=(P(ROW, COL), P(ROW, COL), P(), P()),
        out_specs=(P(ROW, COL, None), P(ROW, COL, None)),
        check_vma=False,
    )
```

time: 267 us -> 112 us (0.42)
  waiting for transfers between devices: 132 us -> 19.4 us
  local copies, waits for them, and re-layouts: 37.5 us -> 2.59 us
  blocking collectives: 36.8 us -> 71.2 us
  starting transfers between devices: 37.5 us -> 3.67 us
  matrix products: 18.8 us -> 0 us
  Pallas kernels: 0 us -> 12.9 us
    all_to_all x6 -> x1, waiting for transfers between devices: 132 us -> 17.7 us  [on_device(): lax.all_to_all(jnp.broadcast_to(share[None], (8, 768, 128)), COL, 0, 0, t...]
    all_to_all x2 -> x3, blocking collectives: 36.8 us -> 71.2 us  [the longest x1 31.5 us: on_device(): arrived = lax.all_to_all(pack(occ, vir, scattered), ROW, 0, 0, tiled=True)]
    all_to_all x6 -> x1, starting transfers between devices: 37.5 us -> 3.58 us  [on_device(): lax.all_to_all(jnp.broadcast_to(share[None], (8, 768, 128)), COL, 0, 0, t...]
    dot_general x12 -> x0, matrix products: 18.8 us -> none  [the longest x10 14.8 us: apply_table(): return jnp.einsum(form, data, table, precision=lax.Precision.HIGHEST)]
    unnamed x18 -> x6, local copies, waits for them, and re-layouts: 18 us -> 1.16 us
    pallas_call x0 -> x4, Pallas kernels: none -> 12.9 us  [the longest x1 4.76 us: finish(): pl.pallas_call(finish_kernel, out_shape=(shape, shape), in_specs=[vmem] *...]
    broadcast_in_dim x10 -> x1, local copies, waits for them, and re-layouts: 6.74 us -> 1.36 us  [on_device(): jnp.broadcast_to(share[None], (8, 768, 128))]
    reshape x4 -> x3, local copies, waits for them, and re-layouts: 5.03 us -> 0.04 us  [the longest x2 0.03 us: by_half(): part = part.reshape(32, 2, count // 2, 128)]
  transfers between devices with their start and end apart: 6 -> 2, of which waited for: 6 -> 2; matrix products, arithmetic and copies ran while one was open for 5% -> 0% of each run, Pallas kernels for 0% -> 0%
where the time goes in v1:
time: 112 us; the launch traced here: 110 us
  blocking collectives  71.2 us (64%)
  waiting for transfers between devices  19.4 us (17%)
  Pallas kernels  12.9 us (12%)
  starting transfers between devices  3.67 us (3%)
  local copies, waits for them, and re-layouts  2.59 us (2%)
    all_to_all x1, blocking collectives, on_device(): arrived = lax.all_to_all(pack(occ, vir, scattered), ROW, 0, 0, tiled=True)  31.5 us
    all_to_all x1, blocking collectives, on_device(): received = lax.all_to_all(messages, SAME_CORE, 0, 0, tiled=True)  27.8 us
    all_to_all x1, waiting for transfers between devices, on_device(): lax.all_to_all(jnp.broadcast_to(share[None], (8, 768, 128)), COL, 0, 0, t...  17.7 us
    all_to_all x1, blocking collectives, on_device(): lax.all_to_all(prepare(row, occ_decay, vir_decay, occ, vir), COL, 0, 0, t...  11.9 us
    pallas_call x1, Pallas kernels, finish(): pl.pallas_call(finish_kernel, out_shape=(shape, shape), in_specs=[vmem] *...  4.76 us
    pallas_call x1, Pallas kernels, polar_messages(): pl.pallas_call(polar_kernel, out_shape=jax.ShapeDtypeStruct((16, 128, 128...  4.53 us
    all_to_all x1, starting transfers between devices, on_device(): lax.all_to_all(jnp.broadcast_to(share[None], (8, 768, 128)), COL, 0, 0, t...  3.58 us
  transfers between devices with their start and end apart: 2, of which 2 were waited for; matrix products, arithmetic and copies ran while one was open for 0% of the time, Pallas kernels for 0%

profile of v1, /device:TPU:32, one launch (start us, length us, event | category | flops | bytes accessed | tf_op | source)
XLA Modules:
  0.0 110.5 jit_solution(16771377728916331091)
XLA Ops:
  0.6 1.6 %prepare.1 = bf16[8,2,24,128]{3,2,1,0:T(8,128)(2,1)} custom-call(s32[1]{0:T(128)} %bitcast.1.place_ref, f32[1024]{0:T(1024)} %occ_decay_ref.1, f32[512]{0:T(512)} %vir_decay_ref.1, bf16[32,4096]{1,0:T(8,128)(2,1)} %occ_ref.3, bf16[16,4096]{1,0:T(8,128)(2,1)} %vir_ref.3), custom_call_target="tpu_custom_call" | custom-call | tf_op jit(solution)/shard_map/prepare/pallas_call | solution.py:98
  2.3 11.9 %all_to_all.20.rows_ref = bf16[8,2,24,128]{3,2,1,0:T(8,128)(2,1)} all-to-all(bf16[8,2,24,128]{3,2,1,0:T(8,128)(2,1)} %prepare.1), channel_id=1, replica_groups=mesh['xh'=2,'z'=8,'c'=2,'xl'=2,'y'=4] {'xl','y'}, dimensions={0} | all-to-all | bytes 196608 | tf_op jit(solution)/shard_map/all_to_all | solution.py:214
  14.2 1.9 %pack.1 = bf16[32,72,128]{2,1,0:T(8,128)(2,1)} custom-call(bf16[32,4096]{1,0:T(8,128)(2,1)} %occ_ref.3, bf16[16,4096]{1,0:T(8,128)(2,1)} %vir_ref.3, bf16[8,2,24,128]{3,2,1,0:T(8,128)(2,1)} %all_to_all.20.rows_ref), custom_call_target="tpu_custom_call" | custom-call | tf_op jit(solution)/shard_map/pack/pallas_call | solution.py:122
  16.1 31.5 %all_to_all.21 = bf16[32,72,128]{2,1,0:T(8,128)(2,1)S(1)} all-to-all(bf16[32,72,128]{2,1,0:T(8,128)(2,1)} %pack.1), channel_id=1, replica_groups=mesh['xh'=2,'z'=8,'c'=2,'xl'=2,'y'=4] {'xh','z','c'}, dimensions={0} | all-to-all | bytes 1179648 | tf_op jit(solution)/shard_map/all_to_all | solution.py:215
  47.7 1.4 %broadcast_in_dim.2 = bf16[8,768,128]{2,1,0:T(8,128)(2,1)} broadcast(bf16[768,128]{1,0:T(8,128)(2,1)S(1)} %pad_maximum_fusion.1), dimensions={1,2} | broadcast | bytes 1769472 | tf_op jit(solution)/shard_map/broadcast_in_dim | solution.py:226
  49.1 3.6 %all-to-all-start.2 = ((bf16[8,768,128]{2,1,0:T(8,128)(2,1)}), bf16[8,768,128]{2,1,0:T(8,128)(2,1)S(1)}, u32[]{:S(2)}, u32[]{:S(2)}) async-start(bf16[8,768,128]{2,1,0:T(8,128)(2,1)} %broadcast_in_dim.2), calls=%async_computation.2 | async-start | bytes 3145728 | tf_op jit(solution)/shard_map/all_to_all | solution.py:226
  52.8 0.0 copy-start.1
  52.8 0.1 collective-permute-start
  52.9 1.7 %collective-permute-done.other_ref = bf16[1536,128]{1,0:T(8,128)(2,1)S(1)} collective-permute-done((bf16[1536,128]{1,0:T(8,128)(2,1)S(1)}, bf16[1536,128]{1,0:T(8,128)(2,1)S(1)}, u32[]{:S(2)}, u32[]{:S(2)}) %collective-permute-start) | collective-permute-done | bytes 393248 | tf_op jit(solution)/shard_map/ppermute | solution.py:225
  54.6 0.0 copy-start.2
  54.6 17.7 %all-to-all-done.2.rows_ref = bf16[8,768,128]{2,1,0:T(8,128)(2,1)S(1)} async-done(((bf16[8,768,128]{2,1,0:T(8,128)(2,1)}), bf16[8,768,128]{2,1,0:T(8,128)(2,1)S(1)}, u32[]{:S(2)}, u32[]{:S(2)}) %all-to-all-start.2) | async-done | bytes 1572896 | tf_op jit(solution)/shard_map/all_to_all | solution.py:226
  72.3 0.0 copy-start
  72.3 0.0 copy-done.1
  72.3 0.0 copy-done.2
  72.3 1.1 %copy-done = bf16[8,768,128]{2,1,0:T(8,128)(2,1)} copy-done((bf16[8,768,128]{2,1,0:T(8,128)(2,1)}, bf16[8,768,128]{2,1,0:T(8,128)(2,1)S(1)}, u32[]{:S(2)}) %copy-start) | copy-done | bytes 1572888
  73.4 4.5 %polar.1 = bf16[16,128,128]{2,1,0:T(8,128)(2,1)} custom-call(s32[1]{0:T(128)} %bitcast.core_ref, bf16[1536,128]{1,0:T(8,128)(2,1)} %copy-done.1, bf16[1536,128]{1,0:T(8,128)(2,1)} %copy-done.2, bf16[8,768,128]{2,1,0:T(8,128)(2,1)} %copy-done, bf16[512,256]{1,0:T(8,128)(2,1)} %constant.30.clone.high_ref, bf16[512,256]{1,0:T(8,128)(2,1)} %constant.31.clone.low_ref), custom_call_target="tpu_custom_call" | custom-call | tf_op jit(solution)/shard_map/polar/pallas_call | solution.py:168
  78.0 27.8 %all_to_all.22 = bf16[128,16,128]{2,1,0:T(8,128)(2,1)} all-to-all(bf16[128,16,128]{2,1,0:T(8,128)(2,1)} %bitcast.17), channel_id=1, replica_groups=mesh['xh'=2,'z'=8,'c'=2,'xl'=2,'y'=4] {'xh','z','xl','y'}, dimensions={0} | all-to-all | bytes 1048576 | tf_op jit(solution)/shard_map/all_to_all | solution.py:228
  105.7 4.8 %finish.1 = (f32[32,4,1024]{2,1,0:T(4,128)}, f32[32,4,1024]{2,1,0:T(4,128)}) custom-call(bf16[2048,128]{1,0:T(8,128)(2,1)} %bitcast.16, bf16[512,512]{1,0:T(8,128)(2,1)} %constant.32.clone.a_high_ref, bf16[512,512]{1,0:T(8,128)(2,1)} %constant.33.clone.a_low_ref, bf16[256,256]{1,0:T(8,128)(2,1)} %constant.34.clone.b_high_ref, ...), custom_call_target="tpu_custom_call" | custom-call | tf_op jit(solution)/shard_map/finish/pallas_call | solution.py:202
  (7 shorter events, 0.1 us)
Async XLA Ops:
  49.1 23.2 %all-to-all-start.2 = ((bf16[8,768,128]{2,1,0:T(8,128)(2,1)}), bf16[8,768,128]{2,1,0:T(8,128)(2,1)S(1)}, u32[]{:S(2)}, u32[]{:S(2)}) async-start(bf16[8,768,128]{2,1,0:T(8,128)(2,1)} %broadcast_in_dim.2), calls=%async_computation.2 | async-start | bytes 3145728 | tf_op jit(solution)/shard_map/all_to_all | solution.py:226
  52.8 19.5 %copy-start.1 = (bf16[1536,128]{1,0:T(8,128)(2,1)}, bf16[1536,128]{1,0:T(8,128)(2,1)S(1)}, u32[]{:S(2)}) copy-start(bf16[1536,128]{1,0:T(8,128)(2,1)S(1)} %pad_maximum_fusion.own_ref) | copy-start | bytes 1179652
  52.8 1.8 %collective-permute-start = (bf16[1536,128]{1,0:T(8,128)(2,1)S(1)}, bf16[1536,128]{1,0:T(8,128)(2,1)S(1)}, u32[]{:S(2)}, u32[]{:S(2)}) collective-permute-start(bf16[1536,128]{1,0:T(8,128)(2,1)S(1)} %pad_maximum_fusion.own_ref), channel_id=1, source_target_pairs={{0,8},{8,0},{1,9},{9,1},{2,10},{10,2},{3,11},{11,3},{4,12},{12,4},... | collective-permute-start | bytes 1179656 | tf_op jit(solution)/shard_map/ppermute | solution.py:225
  54.6 17.7 %copy-start.2 = (bf16[1536,128]{1,0:T(8,128)(2,1)}, bf16[1536,128]{1,0:T(8,128)(2,1)S(1)}, u32[]{:S(2)}) copy-start(bf16[1536,128]{1,0:T(8,128)(2,1)S(1)} %collective-permute-done.other_ref) | copy-start | bytes 1179652
  72.3 1.2 %copy-start = (bf16[8,768,128]{2,1,0:T(8,128)(2,1)}, bf16[8,768,128]{2,1,0:T(8,128)(2,1)S(1)}, u32[]{:S(2)}) copy-start(bf16[8,768,128]{2,1,0:T(8,128)(2,1)S(1)} %all-to-all-done.2.rows_ref) | copy-start | bytes 4718596

commit v2 on v1

--- a/solution.py
+++ b/solution.py
@@ -13,12 +13,25 @@
 NGRID = 32768
 POLAR_FACTOR = -1.0 / math.sqrt(NOCC * NVIR)
 NORMAL = 1.0 / math.sqrt(NGRID)
-FINE = ("xh", "z", "c", "xl", "y")
-FINE_SIZES = (2, 8, 2, 2, 4)
-ROW = ("xh", "z", "c")
-COL = ("xl", "y")
-SAME_CORE = ("xh", "z", "xl", "y")
+Z = ("z2", "z1", "z0")
+Y = ("y1", "y0")
+ROW = ("xh", *Z, "c")
+COL = ("xl", *Y)
+FINE = ROW + COL
+LAST = ("z0", "y0", "y1", "z1", "xh", "xl", "z2")
 BF16 = jnp.bfloat16
+LIMIT = 16 * 1024 * 1024
+
+
+def place_in_last(m, j):
+    bits = dict(zip(("xh", *Z), ((m >> 3) & 1, (m >> 2) & 1, (m >> 1) & 1, m & 1)))
+    bits.update(zip(COL, ((j >> 2) & 1, (j >> 1) & 1, j & 1)))
+    place = 0
+    for axis in LAST:
+        place = 2 * place + bits[axis]
+    return place
+
+
 F32 = jnp.float32
 
 
@@ -111,42 +124,47 @@
     )(place, occ_decay, vir_decay, occ, vir)
 
 
-def pack_kernel(occ_ref, vir_ref, rows_ref, out_ref):
+def pack_kernel(occ_ref, vir_ref, out_ref):
     for p in range(32):
         out_ref[p, 0:32, :] = occ_ref[:, 128 * p : 128 * (p + 1)]
         out_ref[p, 32:48, :] = vir_ref[:, 128 * p : 128 * (p + 1)]
-        out_ref[p, 48:72, :] = rows_ref[0, p % 2]
-
-
-def pack(occ, vir, rows):
+
+
+def pack(occ, vir):
+    vmem = pl.BlockSpec(memory_space=pltpu.VMEM)
     return pl.pallas_call(
         pack_kernel,
-        grid=(1,),
-        out_shape=jax.ShapeDtypeStruct((32, 72, 128), BF16),
-        in_specs=[
-            pl.BlockSpec((32, 4096), lambda i: (0, 0)),
-            pl.BlockSpec((16, 4096), lambda i: (0, 0)),
-            pl.BlockSpec((1, 2, 24, 128), lambda i: (0, 0, 0, 0)),
-        ],
-        out_specs=pl.BlockSpec((32, 72, 128), lambda i: (0, 0, 0)),
+        out_shape=jax.ShapeDtypeStruct((32, 48, 128), BF16),
+        in_specs=[vmem, vmem],
+        out_specs=vmem,
+        compiler_params=pltpu.CompilerParams(vmem_limit_bytes=LIMIT),
         name="pack",
-    )(occ, vir, rows)
-
-
-def polar_kernel(core_ref, own_ref, other_ref, rows_ref, high_ref, low_ref, out_ref, polar_ref):
-    core = core_ref[0]
-    for half, ref in enumerate((own_ref, other_ref)):
-        start = pl.multiple_of((core if half == 0 else 1 - core) * 128, 128)
-        occ = ref[0:1024, :].T
-        vir = ref[1024:1536, :].T
-        for y in range(4):
-            green_occ = dot(occ[:, :512], rows_ref[y, :512]) + dot(
-                occ[:, 512:], rows_ref[4 + y, :512]
+    )(occ, vir)
+
+
+def polar_kernel(place_ref, own_ref, other_ref, near_ref, *refs):
+    step_refs, (up_ref, down_ref, high_ref, low_ref, out_ref, polar_ref) = refs[:3], refs[3:]
+    core, xl, y = place_ref[0], place_ref[1], place_ref[2]
+    near = (near_ref, *step_refs)
+    points = []
+    for ref in (own_ref, other_ref):
+        halves = []
+        for half in (xl, 1 - xl):
+            occ = ref[pl.ds(pl.multiple_of(half * 512, 512), 512), :].T
+            vir = ref[pl.ds(pl.multiple_of(1024 + half * 256, 256), 256), :].T
+            halves.append((occ, vir))
+        points.append(halves)
+    for step in range(4):
+        far_ref = up_ref if step < 2 else down_ref
+        base = 768 * (step % 2)
+        for which, halves in enumerate(points):
+            start = pl.multiple_of((core if which == 0 else 1 - core) * 128, 128)
+            (occ_near, vir_near), (occ_far, vir_far) = halves
+            green_occ = dot(occ_near, near[step][:512]) + dot(occ_far, far_ref[base : base + 512])
+            green_vir = dot(vir_near, near[step][512:]) + dot(
+                vir_far, far_ref[base + 512 : base + 768]
             )
-            green_vir = dot(vir[:, :256], rows_ref[y, 512:]) + dot(
-                vir[:, 256:], rows_ref[4 + y, 512:]
-            )
-            polar_ref[pl.ds(start, 128), 128 * y : 128 * (y + 1)] = (
+            polar_ref[pl.ds(start, 128), 128 * step : 128 * (step + 1)] = (
                 green_occ * green_vir * POLAR_FACTOR
             )
     polar = polar_ref[...]
@@ -157,22 +175,26 @@
         + dot(high_ref[...], polar_low)
         + dot(low_ref[...], polar_high)
     )
-    for m in range(16):
-        pieces = [spectrum[128 * i : 128 * (i + 1), 32 * m : 32 * (m + 1)] for i in range(4)]
-        out_ref[m] = jnp.concatenate(pieces, axis=1).astype(BF16)
-
-
-def polar_messages(core, own, other, rows):
+    for step in range(4):
+        chunk = lax.rem(y + 4 - step, 4)
+        for u in range(4):
+            lane = 128 * step + 32 * u
+            pieces = [spectrum[128 * i : 128 * (i + 1), lane : lane + 32] for i in range(4)]
+            out_ref[4 * chunk + u] = jnp.concatenate(pieces, axis=1).astype(BF16)
+
+
+def polar_messages(place, *arrays):
     high, low = c_table()
     vmem = pl.BlockSpec(memory_space=pltpu.VMEM)
     return pl.pallas_call(
         polar_kernel,
         out_shape=jax.ShapeDtypeStruct((16, 128, 128), BF16),
-        in_specs=[pl.BlockSpec(memory_space=pltpu.SMEM)] + [vmem] * 5,
+        in_specs=[pl.BlockSpec(memory_space=pltpu.SMEM)] + [vmem] * 10,
         out_specs=vmem,
         scratch_shapes=[pltpu.VMEM((256, 512), F32)],
+        compiler_params=pltpu.CompilerParams(vmem_limit_bytes=LIMIT),
         name="polar",
-    )(core, own, other, rows, high, low)
+    )(place, *arrays, high, low)
 
 
 def finish_kernel(x_ref, a_high_ref, a_low_ref, b_high_ref, b_low_ref, real_ref, imag_ref):
@@ -204,33 +226,47 @@
         out_shape=(shape, shape),
         in_specs=[vmem] * 5,
         out_specs=(vmem, vmem),
+        compiler_params=pltpu.CompilerParams(vmem_limit_bytes=LIMIT),
         name="finish",
     )(x, *a_table(), *b_table())
 
 
+def shift(x, axes, count, by):
+    return lax.ppermute(x, axes, [(i, (i + by) % count) for i in range(count)])
+
+
 def on_device(occ, vir, occ_decay, vir_decay):
     row = lax.axis_index(ROW).astype(jnp.int32).reshape(1)
-    core = lax.axis_index("c").astype(jnp.int32).reshape(1)
+    place = jnp.stack([lax.axis_index(a).astype(jnp.int32) for a in ("c", "xl", Y)])
     scattered = lax.all_to_all(prepare(row, occ_decay, vir_decay, occ, vir), COL, 0, 0, tiled=True)
-    arrived = lax.all_to_all(pack(occ, vir, scattered), ROW, 0, 0, tiled=True)
+    share = jnp.broadcast_to(scattered[0][None], (16, 2, 24, 128)).reshape(32, 24, 128)
+    share = lax.all_to_all(share, ROW, 0, 0, tiled=True)
+    arrived = lax.all_to_all(pack(occ, vir), ROW, 0, 0, tiled=True)
+
+    near = jnp.concatenate([share[:, :16].reshape(512, 128), share[:, 16:].reshape(256, 128)], axis=0)
+    steps = [shift(near, Y, 4, by) for by in (1, 2, 3)]
+    up = shift(jnp.concatenate([near, steps[0]], axis=0), ("xh", "xl"), 4, 1)
+    down = shift(jnp.concatenate([steps[1], steps[2]], axis=0), ("xh", "xl"), 4, -1)
 
     def by_half(part, count):
         part = part.reshape(32, 2, count // 2, 128)
         return jnp.transpose(part, (1, 0, 2, 3)).reshape(32 * count, 128)
 
-    own = jnp.concatenate([by_half(arrived[:, :32], 32), by_half(arrived[:, 32:48], 16)], axis=0)
-    share = jnp.concatenate(
-        [arrived[:, 48:64].reshape(512, 128), arrived[:, 64:72].reshape(256, 128)], axis=0
-    )
+    own = jnp.concatenate([by_half(arrived[:, :32], 32), by_half(arrived[:, 32:], 16)], axis=0)
     other = lax.ppermute(own, "c", [(0, 1), (1, 0)])
-    rows = lax.all_to_all(jnp.broadcast_to(share[None], (8, 768, 128)), COL, 0, 0, tiled=True)
-    messages = polar_messages(core, own, other, rows).reshape(128, 16, 128)
-    received = lax.all_to_all(messages, SAME_CORE, 0, 0, tiled=True)
-    return finish(received.reshape(2048, 128))
+    messages = polar_messages(place, own, other, near, *steps, up, down).reshape(16, 8, 16, 128)
+
+    bits = messages.reshape(2, 2, 2, 2, 2, 2, 2, 16, 128)
+    names = ("xh", *Z, *COL)
+    to_last = [names.index(a) for a in LAST]
+    sent = jnp.transpose(bits, (*to_last, 7, 8)).reshape(128, 16, 128)
+    received = lax.all_to_all(sent, LAST, 0, 0, tiled=True).reshape(bits.shape)
+    back = [LAST.index(a) for a in names]
+    return finish(jnp.transpose(received, (*back, 7, 8)).reshape(2048, 128))
 
 
 def solution(mesh):
-    fine = Mesh(mesh.devices.reshape(FINE_SIZES), FINE)
+    fine = Mesh(mesh.devices.reshape((2,) * len(FINE)), FINE)
     return jax.shard_map(
         on_device,
         mesh=fine,

time: 112 us -> 107 us (0.955); the launches traced: 110 us -> 107 us
  blocking collectives: 71.2 us -> 41.7 us
  starting transfers between devices: 3.67 us -> 21.4 us
  waiting for transfers between devices: 19.4 us -> 31.6 us
  Pallas kernels: 12.9 us -> 8.35 us
    all_to_all x2 -> x1, blocking collectives: 59.3 us -> 29.9 us  [on_device(): received = lax.all_to_all(sent, LAST, 0, 0, tiled=True).reshape(bits.shape)]
    ppermute x0 -> x5, waiting for transfers between devices: none -> 18.4 us  [shift(): return lax.ppermute(x, axes, [(i, (i + by) % count) for i in range(count)])]
    all_to_all x1 -> x2, starting transfers between devices: 3.58 us -> 15.9 us  [the longest x1 11 us: on_device(): share = lax.all_to_all(share, ROW, 0, 0, tiled=True)]
    ppermute x0 -> x5, starting transfers between devices: none -> 5.45 us  [shift(): return lax.ppermute(x, axes, [(i, (i + by) % count) for i in range(count)])]
    all_to_all x1 -> x2, waiting for transfers between devices: 17.7 us -> 13.2 us  [the longest x1 11.4 us: on_device(): share = lax.all_to_all(share, ROW, 0, 0, tiled=True)]
    pallas_call x1, Pallas kernels: 4.53 us -> 2.54 us  [polar_messages(): pl.pallas_call(polar_kernel, out_shape=jax.ShapeDtypeStruct((16, 128, 128...]
    ppermute x1, waiting for transfers between devices: 1.71 us -> 0.01 us  [on_device(): other = lax.ppermute(own, 'c', [(0, 1), (1, 0)])]
    pallas_call x1, Pallas kernels: 4.76 us -> 3.35 us  [finish(): pl.pallas_call(finish_kernel, out_shape=(shape, shape), in_specs=[vmem] *...]
  transfers between devices with their start and end apart: 2 -> 8, of which waited for: 2 -> 7; matrix products, arithmetic and copies ran while one was open for 0% -> 1% of each run, Pallas kernels for 0% -> 1%
where the time goes in v2:
time: 107 us
  blocking collectives  41.7 us (39%)
  waiting for transfers between devices  31.6 us (30%)
  starting transfers between devices  21.4 us (20%)
  Pallas kernels  8.35 us (8%)
  local copies, waits for them, and re-layouts  2.04 us (2%)
    all_to_all x1, blocking collectives, on_device(): received = lax.all_to_all(sent, LAST, 0, 0, tiled=True).reshape(bits.shape)  29.9 us
    ppermute x5, waiting for transfers between devices, shift(): return lax.ppermute(x, axes, [(i, (i + by) % count) for i in range(count)])  18.4 us
    all_to_all x1, blocking collectives, on_device(): lax.all_to_all(prepare(row, occ_decay, vir_decay, occ, vir), COL, 0, 0, t...  11.8 us
    all_to_all x1, waiting for transfers between devices, on_device(): share = lax.all_to_all(share, ROW, 0, 0, tiled=True)  11.4 us
    all_to_all x1, starting transfers between devices, on_device(): share = lax.all_to_all(share, ROW, 0, 0, tiled=True)  11 us
    ppermute x5, starting transfers between devices, shift(): return lax.ppermute(x, axes, [(i, (i + by) % count) for i in range(count)])  5.45 us
    all_to_all x1, starting transfers between devices, on_device(): arrived = lax.all_to_all(pack(occ, vir), ROW, 0, 0, tiled=True)  4.86 us
    pallas_call x1, Pallas kernels, finish(): pl.pallas_call(finish_kernel, out_shape=(shape, shape), in_specs=[vmem] *...  3.35 us
  transfers between devices with their start and end apart: 8, of which 7 were waited for; matrix products, arithmetic and copies ran while one was open for 1% of the time, Pallas kernels for 1%

profile of v2, /device:TPU:32, one launch (start us, length us, event | category | flops | bytes accessed | tf_op | source)
XLA Modules:
  0.0 106.9 jit_solution(15136232639618678151)
XLA Ops:
  0.6 1.6 %prepare.1 = bf16[8,2,24,128]{3,2,1,0:T(8,128)(2,1)} custom-call(s32[1]{0:T(128)} %bitcast.9.place_ref, f32[1024]{0:T(1024)} %occ_decay_ref.1, f32[512]{0:T(512)} %vir_decay_ref.1, bf16[32,4096]{1,0:T(8,128)(2,1)} %occ_ref.3, bf16[16,4096]{1,0:T(8,128)(2,1)} %vir_ref.3), custom_call_target="tpu_custom_call" | custom-call | tf_op jit(solution)/shard_map/prepare/pallas_call | solution.py:111
  2.3 11.8 %all_to_all.20 = bf16[8,2,24,128]{3,2,1,0:T(8,128)(2,1)S(1)} all-to-all(bf16[8,2,24,128]{3,2,1,0:T(8,128)(2,1)} %prepare.1), channel_id=1, replica_groups=mesh['xh'=2,'z2'=2,'z1'=2,'z0'=2,'c'=2,'xl'=2,'y1'=2,'y0'=2] {'xl','y1',..., dimensions={0} | all-to-all | bytes 196608 | tf_op jit(solution)/shard_map/all_to_all | solution.py:241
  14.1 0.0 copy-start
  14.1 0.7 broadcast_in_dim.8
  14.8 0.0 copy-start.3
  14.8 11.0 %all-to-all-start.2 = ((bf16[32,24,128]{2,1,0:T(8,128)(2,1)}), bf16[32,24,128]{2,1,0:T(8,128)(2,1)S(1)}, u32[]{:S(2)}, u32[]{:S(2)}) async-start(bf16[32,24,128]{2,1,0:T(8,128)(2,1)} %bitcast.11), calls=%async_computation.2 | async-start | bytes 393216 | tf_op jit(solution)/shard_map/all_to_all | solution.py:243
  25.9 0.0 copy-done
  25.9 0.0 copy-done.3
  25.9 0.8 pack.1
  26.7 11.4 %all-to-all-done.2 = bf16[32,24,128]{2,1,0:T(8,128)(2,1)S(1)} async-done(((bf16[32,24,128]{2,1,0:T(8,128)(2,1)}), bf16[32,24,128]{2,1,0:T(8,128)(2,1)S(1)}, u32[]{:S(2)}, u32[]{:S(2)}) %all-to-all-start.2) | async-done | bytes 196640 | tf_op jit(solution)/shard_map/all_to_all | solution.py:243
  38.1 4.9 %all-to-all-start = ((bf16[32,48,128]{2,1,0:T(8,128)(2,1)}), bf16[32,48,128]{2,1,0:T(8,128)(2,1)S(1)}, u32[]{:S(2)}, u32[]{:S(2)}) async-start(bf16[32,48,128]{2,1,0:T(8,128)(2,1)} %pack.1), calls=%async_computation | async-start | bytes 786432 | tf_op jit(solution)/shard_map/all_to_all | solution.py:244
  43.0 1.2 %collective-permute-start.3 = (bf16[768,128]{1,0:T(8,128)(2,1)S(1)}, bf16[768,128]{1,0:T(8,128)(2,1)S(1)}, u32[]{:S(2)}, u32[]{:S(2)}) collective-permute-start(bf16[768,128]{1,0:T(8,128)(2,1)S(1)} %pad_maximum_fusion.3.near_ref), channel_id=1, source_target_pairs={{0,3},{1,0},{2,1},{3,2},{4,7},{5,4},{6,5},{7,6},{8,11},{9,8},{10,9... | collective-permute-start | bytes 589832 | tf_op jit(solution)/shard_map/ppermute | solution.py:235
  44.2 1.5 %collective-permute-start.2 = (bf16[768,128]{1,0:T(8,128)(2,1)S(1)}, bf16[768,128]{1,0:T(8,128)(2,1)S(1)}, u32[]{:S(2)}, u32[]{:S(2)}) collective-permute-start(bf16[768,128]{1,0:T(8,128)(2,1)S(1)} %pad_maximum_fusion.3.near_ref), channel_id=1, source_target_pairs={{0,2},{1,3},{2,0},{3,1},{4,6},{5,7},{6,4},{7,5},{8,10},{9,11},{10,... | collective-permute-start | bytes 589832 | tf_op jit(solution)/shard_map/ppermute | solution.py:235
  45.7 0.0 collective-permute-start.1
  45.7 5.1 %collective-permute-done.3.refs_2_ = bf16[768,128]{1,0:T(8,128)(2,1)S(1)} collective-permute-done((bf16[768,128]{1,0:T(8,128)(2,1)S(1)}, bf16[768,128]{1,0:T(8,128)(2,1)S(1)}, u32[]{:S(2)}, u32[]{:S(2)}) %collective-permute-start.3) | collective-permute-done | bytes 196640 | tf_op jit(solution)/shard_map/ppermute | solution.py:235
  50.8 2.7 %collective-permute-done.2.refs_1_ = bf16[768,128]{1,0:T(8,128)(2,1)S(1)} collective-permute-done((bf16[768,128]{1,0:T(8,128)(2,1)S(1)}, bf16[768,128]{1,0:T(8,128)(2,1)S(1)}, u32[]{:S(2)}, u32[]{:S(2)}) %collective-permute-start.2) | collective-permute-done | bytes 196640 | tf_op jit(solution)/shard_map/ppermute | solution.py:235
  53.6 2.5 %collective-permute-start.5 = (bf16[1536,128]{1,0:T(8,128)(2,1)S(1)}, bf16[1536,128]{1,0:T(8,128)(2,1)S(1)}, u32[]{:S(2)}, u32[]{:S(2)}) collective-permute-start(bf16[1536,128]{1,0:T(8,128)(2,1)S(1)} %pad_maximum_fusion.2), channel_id=1, source_target_pairs={{0,132},{4,0},{128,4},{132,128},{1,133},{5,1},{129,5},{133,129},{2... | collective-permute-start | bytes 1179656 | tf_op jit(solution)/shard_map/ppermute | solution.py:235
  56.1 0.5 collective-permute-done.1.refs_0_
  56.6 0.8 pad_maximum_fusion.1
  57.4 0.2 collective-permute-start.4
  57.6 1.9 %all-to-all-done = bf16[32,48,128]{2,1,0:T(8,128)(2,1)S(1)} async-done(((bf16[32,48,128]{2,1,0:T(8,128)(2,1)}), bf16[32,48,128]{2,1,0:T(8,128)(2,1)S(1)}, u32[]{:S(2)}, u32[]{:S(2)}) %all-to-all-start) | async-done | bytes 393248 | tf_op jit(solution)/shard_map/all_to_all | solution.py:244
  59.6 0.0 copy-start.4
  59.6 0.0 copy-start.5
  59.6 0.1 collective-permute-start
  59.7 0.1 pad_add_fusion.place_ref
  59.8 3.1 %collective-permute-done.5.refs_4_ = bf16[1536,128]{1,0:T(8,128)(2,1)S(1)} collective-permute-done((bf16[1536,128]{1,0:T(8,128)(2,1)S(1)}, bf16[1536,128]{1,0:T(8,128)(2,1)S(1)}, u32[]{:S(2)}, u32[]{:S(2)}) %collective-permute-start.5) | collective-permute-done | bytes 393248 | tf_op jit(solution)/shard_map/ppermute | solution.py:235
  62.9 6.9 %collective-permute-done.4.refs_3_ = bf16[1536,128]{1,0:T(8,128)(2,1)S(1)} collective-permute-done((bf16[1536,128]{1,0:T(8,128)(2,1)}, bf16[1536,128]{1,0:T(8,128)(2,1)S(1)}, u32[]{:S(2)}, u32[]{:S(2)}) %collective-permute-start.4) | collective-permute-done | bytes 393248 | tf_op jit(solution)/shard_map/ppermute | solution.py:235
  69.8 0.0 collective-permute-done.other_ref
  69.8 0.0 copy-done.4
  69.8 0.0 copy-done.5
  69.8 2.5 %polar.1 = bf16[16,128,128]{2,1,0:T(8,128)(2,1)S(1)} custom-call(s32[3]{0:T(128)S(1)} %pad_add_fusion.place_ref, bf16[1536,128]{1,0:T(8,128)(2,1)S(1)} %pad_maximum_fusion.own_ref, bf16[1536,128]{1,0:T(8,128)(2,1)S(1)} %collective-permute-done.other_ref, bf16[768,128]{1,0:T(8,128)(2,1)S(1)} %pad_maximum_fusion.3.near_ref, ...), custom_call_target="tpu_custom_call" | custom-call | tf_op jit(solution)/shard_map/polar/pallas_call | solution.py:189
  72.4 0.1 copy.16
  72.5 0.0 copy-start.6
  72.5 0.0 copy-start.7
  72.5 29.9 %all_to_all.21 = bf16[128,16,128]{2,1,0:T(8,128)(2,1)S(1)} all-to-all(bf16[128,16,128]{2,1,0:T(8,128)(2,1)S(1)} %bitcast.29), channel_id=1, replica_groups=mesh['xh'=2,'z2'=2,'z1'=2,'z0'=2,'c'=2,'xl'=2,'y1'=2,'y0'=2] {'z0','y0',..., dimensions={0} | all-to-all | bytes 1048576 | tf_op jit(solution)/shard_map/all_to_all | solution.py:263
  102.3 0.0 copy-start.1
  102.3 0.0 copy-start.2
  102.4 0.1 copy.17
  102.4 0.0 copy-done.6
  102.4 0.0 copy-done.7
  102.4 1.0 copy-done.1
  103.4 0.2 copy-done.2
  103.5 3.3 %finish.1 = (f32[32,4,1024]{2,1,0:T(4,128)}, f32[32,4,1024]{2,1,0:T(4,128)}) custom-call(bf16[2048,128]{1,0:T(8,128)(2,1)S(1)} %bitcast.27, bf16[512,512]{1,0:T(8,128)(2,1)S(1)} %copy-done.2, bf16[512,512]{1,0:T(8,128)(2,1)S(1)} %copy-done.1, bf16[256,256]{1,0:T(8,128)(2,1)S(1)} %copy-done.7, bf16[256,256]{1,0:T(8,128)(2,1)S(1)} %copy-done.6), custom_call_target="tpu_custom_call" | custom-call | tf_op jit(solution)/shard_map/finish/pallas_call | solution.py:224
  (10 shorter events, 0.1 us)
Async XLA Ops:
  14.1 11.7 %copy-start = (bf16[32,4096]{1,0:T(8,128)(2,1)S(1)}, bf16[32,4096]{1,0:T(8,128)(2,1)}, u32[]{:S(2)}) copy-start(bf16[32,4096]{1,0:T(8,128)(2,1)} %occ_ref.3) | copy-start | bytes 786436
  14.8 11.0 %copy-start.3 = (bf16[16,4096]{1,0:T(8,128)(2,1)S(1)}, bf16[16,4096]{1,0:T(8,128)(2,1)}, u32[]{:S(2)}) copy-start(bf16[16,4096]{1,0:T(8,128)(2,1)} %vir_ref.3) | copy-start | bytes 393220
  14.8 23.2 %all-to-all-start.2 = ((bf16[32,24,128]{2,1,0:T(8,128)(2,1)}), bf16[32,24,128]{2,1,0:T(8,128)(2,1)S(1)}, u32[]{:S(2)}, u32[]{:S(2)}) async-start(bf16[32,24,128]{2,1,0:T(8,128)(2,1)} %bitcast.11), calls=%async_computation.2 | async-start | bytes 393216 | tf_op jit(solution)/shard_map/all_to_all | solution.py:243
  38.1 21.4 %all-to-all-start = ((bf16[32,48,128]{2,1,0:T(8,128)(2,1)}), bf16[32,48,128]{2,1,0:T(8,128)(2,1)S(1)}, u32[]{:S(2)}, u32[]{:S(2)}) async-start(bf16[32,48,128]{2,1,0:T(8,128)(2,1)} %pack.1), calls=%async_computation | async-start | bytes 786432 | tf_op jit(solution)/shard_map/all_to_all | solution.py:244
  43.0 7.9 %collective-permute-start.3 = (bf16[768,128]{1,0:T(8,128)(2,1)S(1)}, bf16[768,128]{1,0:T(8,128)(2,1)S(1)}, u32[]{:S(2)}, u32[]{:S(2)}) collective-permute-start(bf16[768,128]{1,0:T(8,128)(2,1)S(1)} %pad_maximum_fusion.3.near_ref), channel_id=1, source_target_pairs={{0,3},{1,0},{2,1},{3,2},{4,7},{5,4},{6,5},{7,6},{8,11},{9,8},{10,9... | collective-permute-start | bytes 589832 | tf_op jit(solution)/shard_map/ppermute | solution.py:235
  44.2 9.3 %collective-permute-start.2 = (bf16[768,128]{1,0:T(8,128)(2,1)S(1)}, bf16[768,128]{1,0:T(8,128)(2,1)S(1)}, u32[]{:S(2)}, u32[]{:S(2)}) collective-permute-start(bf16[768,128]{1,0:T(8,128)(2,1)S(1)} %pad_maximum_fusion.3.near_ref), channel_id=1, source_target_pairs={{0,2},{1,3},{2,0},{3,1},{4,6},{5,7},{6,4},{7,5},{8,10},{9,11},{10,... | collective-permute-start | bytes 589832 | tf_op jit(solution)/shard_map/ppermute | solution.py:235
  45.7 10.9 %collective-permute-start.1 = (bf16[768,128]{1,0:T(8,128)(2,1)S(1)}, bf16[768,128]{1,0:T(8,128)(2,1)S(1)}, u32[]{:S(2)}, u32[]{:S(2)}) collective-permute-start(bf16[768,128]{1,0:T(8,128)(2,1)S(1)} %pad_maximum_fusion.3.near_ref), channel_id=1, source_target_pairs={{0,1},{1,2},{2,3},{3,0},{4,5},{5,6},{6,7},{7,4},{8,9},{9,10},{10,1... | collective-permute-start | bytes 589832 | tf_op jit(solution)/shard_map/ppermute | solution.py:235
  53.6 9.3 %collective-permute-start.5 = (bf16[1536,128]{1,0:T(8,128)(2,1)S(1)}, bf16[1536,128]{1,0:T(8,128)(2,1)S(1)}, u32[]{:S(2)}, u32[]{:S(2)}) collective-permute-start(bf16[1536,128]{1,0:T(8,128)(2,1)S(1)} %pad_maximum_fusion.2), channel_id=1, source_target_pairs={{0,132},{4,0},{128,4},{132,128},{1,133},{5,1},{129,5},{133,129},{2... | collective-permute-start | bytes 1179656 | tf_op jit(solution)/shard_map/ppermute | solution.py:235
  57.4 12.5 %collective-permute-start.4 = (bf16[1536,128]{1,0:T(8,128)(2,1)}, bf16[1536,128]{1,0:T(8,128)(2,1)S(1)}, u32[]{:S(2)}, u32[]{:S(2)}) collective-permute-start(bf16[1536,128]{1,0:T(8,128)(2,1)} %pad_maximum_fusion.1), channel_id=1, source_target_pairs={{0,4},{4,128},{128,132},{132,0},{1,5},{5,129},{129,133},{133,1},{2... | collective-permute-start | bytes 1179656 | tf_op jit(solution)/shard_map/ppermute | solution.py:235
  59.6 10.3 %copy-start.4 = (bf16[512,256]{1,0:T(8,128)(2,1)S(1)}, bf16[512,256]{1,0:T(8,128)(2,1)}, u32[]{:S(2)}) copy-start(bf16[512,256]{1,0:T(8,128)(2,1)} %constant.51.clone.refs_6_) | copy-start | bytes 786436
  59.6 10.3 %copy-start.5 = (bf16[512,256]{1,0:T(8,128)(2,1)S(1)}, bf16[512,256]{1,0:T(8,128)(2,1)}, u32[]{:S(2)}) copy-start(bf16[512,256]{1,0:T(8,128)(2,1)} %constant.50.clone.refs_5_) | copy-start | bytes 786436
  59.6 10.2 %collective-permute-start = (bf16[1536,128]{1,0:T(8,128)(2,1)S(1)}, bf16[1536,128]{1,0:T(8,128)(2,1)S(1)}, u32[]{:S(2)}, u32[]{:S(2)}) collective-permute-start(bf16[1536,128]{1,0:T(8,128)(2,1)S(1)} %pad_maximum_fusion.own_ref), channel_id=1, source_target_pairs={{0,8},{8,0},{1,9},{9,1},{2,10},{10,2},{3,11},{11,3},{4,12},{12,4},... | collective-permute-start | bytes 1179656 | tf_op jit(solution)/shard_map/ppermute | solution.py:256
  72.5 30.0 %copy-start.6 = (bf16[256,256]{1,0:T(8,128)(2,1)S(1)}, bf16[256,256]{1,0:T(8,128)(2,1)}, u32[]{:S(2)}) copy-start(bf16[256,256]{1,0:T(8,128)(2,1)} %constant.55.clone.b_low_ref) | copy-start | bytes 393220
  72.5 30.0 %copy-start.7 = (bf16[256,256]{1,0:T(8,128)(2,1)S(1)}, bf16[256,256]{1,0:T(8,128)(2,1)}, u32[]{:S(2)}) copy-start(bf16[256,256]{1,0:T(8,128)(2,1)} %constant.54.clone.b_high_ref) | copy-start | bytes 393220
  102.3 1.0 copy-start.1
  102.3 1.2 %copy-start.2 = (bf16[512,512]{1,0:T(8,128)(2,1)S(1)}, bf16[512,512]{1,0:T(8,128)(2,1)}, u32[]{:S(2)}) copy-start(bf16[512,512]{1,0:T(8,128)(2,1)} %constant.52.clone.a_high_ref) | copy-start | bytes 1572868
